TPU v7x, 128 devices: a whole 4x4x4 slice. The times are simulated.
128 devices in a mesh: row: 8 (over z, core), col: 16 (over y, x).
Axes of the slice: x: 4, y: 4, z: 4, core: 2. Of those that a mesh axis runs over, the one named last changes fastest.
Arguments:
- src_field: bfloat16 [64, 4194304], P(None, ('row', 'col')), may hold values from 0.5 to 2
- src_area: float32 [4194304], P(('row', 'col')), may hold values from 0.3 to 3
- tgt_area: float32 [1048576], P(('row', 'col')), may hold values from 0.3 to 3
- weights: bfloat16 [49152, 128, 128], P(('row', 'col')), may hold values from 0 to 0.0025939941
- send_index: int32 [128, 128, 2], P(('row', 'col')), may hold values from -1 to 255, as said below
- pair_slot: int32 [49152], P(('row', 'col')), may hold values from 0 to 255, as said below
- pair_target: int32 [49152], P(('row', 'col')), may hold values from 0 to 63, as said below
Outputs:
- target_field: float32 [64, 1048576], P(None, ('row', 'col'))
Inputs may be any that keep to these rules, and one draw needn't show every extreme that they name: `send_index`: in each [s, r] the live entries (not -1) come first and there are 1 to 2 of them; every sender sends to every receiver; for each receiver some sender fills all 2 slots. `pair_slot`: each pair of device r names a live slot of what device r receives; every live slot is named by some pair of device r. `pair_target`: every local target block of a device is named by some pair of that device.
All inputs are finite; a program needn't handle non-finite values.
Results may differ from a plain program's by a relative error of at most 0.0003.
Values may be sent and summed in bfloat16 or wider, within the bound.
A program may use at most 128 MiB of HBM per device.

v0:
```python
import jax
import jax.numpy as jnp
from jax import lax
from jax.sharding import Mesh
from jax.sharding import PartitionSpec as P

ROW_COL = ("row_0", "row_1", "col_0", "col_1")


def by_axis(value, axes):
    for axis in axes:
        value = lax.psum(value, axis)
    return value


def shards(src_field, src_area, tgt_area, weights, send_index, pair_slot, pair_target):
    columns, cell_count = src_field.shape
    block_size = weights.shape[1]
    local_blocks = cell_count // block_size
    target_blocks = tgt_area.shape[0] // block_size
    send_rows = send_index[0]
    peer_count, capacity = send_rows.shape
    blocks = src_field.reshape(columns, local_blocks, block_size)
    source_local = jnp.sum(src_field.astype(jnp.float32) * src_area[None, :], axis=1)
    chosen = jnp.maximum(send_rows.reshape(-1), 0)
    outbound = jnp.take(blocks, chosen, axis=1)
    outbound = jnp.transpose(outbound, (1, 0, 2)).reshape(peer_count, capacity, columns, block_size)
    inbound = lax.all_to_all(outbound, ROW_COL, split_axis=0, concat_axis=0, tiled=True)
    inbound = inbound.reshape(peer_count * capacity, columns, block_size)
    picked = jnp.take(inbound, pair_slot, axis=0)
    products = jnp.einsum("pcs,pst->pct", picked, weights, preferred_element_type=jnp.float32)
    placed = jax.ops.segment_sum(products, pair_target, num_segments=target_blocks)
    regridded = jnp.transpose(placed, (1, 0, 2)).reshape(columns, target_blocks * block_size)
    target_local = jnp.sum(regridded * tgt_area[None, :], axis=1)
    source_mass, target_mass = (by_axis(source_local, ROW_COL), by_axis(target_local, ROW_COL))
    return regridded * (source_mass / target_mass)[:, None]


def solution(mesh):
    split = Mesh(mesh.devices.reshape(4, 2, 4, 4), ("row_0", "row_1", "col_0", "col_1"))
    placed = (
        P(None, ROW_COL),
        P(ROW_COL),
        P(ROW_COL),
        P(ROW_COL, None, None),
        P(ROW_COL, None, None),
        P(ROW_COL),
        P(ROW_COL),
    )
    return jax.shard_map(
        shards, mesh=split, in_specs=placed, out_specs=P(None, ROW_COL), check_vma=False
    )
```

profile of v0, /device:TPU:0, one launch (start us, length us, event | category | flops | bytes accessed | tf_op | source)
XLA Modules:
  0.0 171.6 jit_solution(789475034657432095)
XLA Ops:
  0.0 0.7 broadcast_maximum_fusion
  0.7 0.7 broadcast_compare_fusion
  1.4 5.3 %copy_bitcast_fusion = bf16[64,256,128]{2,0,1:T(8,128)(2,1)} fusion(bf16[64,32768]{1,0:T(8,128)(2,1)} %param.7), kind=kLoop, calls=%fused_computation.7 | loop fusion | bytes 8388608 | tf_op jit(solution)/shard_map/reshape | solution.py:23
  6.7 0.1 copy.11
  6.8 0.1 reshape.53
  7.0 0.1 copy.10
  7.1 0.1 le.27
  7.2 5.3 %gather_fusion = bf16[256,64,128]{2,1,0:T(8,128)(2,1)} fusion(bf16[64,256,128]{2,0,1:T(8,128)(2,1)} %copy_bitcast_fusion, s32[1024]{0:T(1024)S(1)} %pad_clamp_fusion.1), kind=kCustom, calls=%fused_computation | custom fusion | bytes 8389632 | tf_op jit(solution)/shard_map/jit(_take)/gather | solution.py:26
  12.5 4.0 %broadcast_select_fusion = bf16[256,64,128]{2,1,0:T(8,128)(2,1)} fusion(bf16[256,64,128]{2,1,0:T(8,128)(2,1)} %gather_fusion, pred[256]{0:T(512)(128)(4,1)S(1)} %le.27), kind=kLoop, calls=%fused_computation.8 | loop fusion | flops 2097152 | bytes 8388864 | tf_op jit(solution)/shard_map/jit(_take)/select_n | solution.py:26
  16.5 0.0 copy-start.2
  16.5 0.0 copy-start
  16.5 11.7 %all-to-all-start = ((bf16[128,2,64,128]{3,2,1,0:T(8,128)(2,1)}), bf16[128,2,64,128]{3,2,1,0:T(8,128)(2,1)}, u32[]{:S(2)}, u32[]{:S(2)}) async-start(bf16[128,2,64,128]{3,2,1,0:T(8,128)(2,1)} %bitcast.18), calls=%async_computation | async-start | bytes 8388608 | tf_op jit(solution)/shard_map/all_to_all | solution.py:28
  28.2 0.0 copy-done.2
  28.3 0.0 copy-done
  28.3 3.1 %multiply_reduce_fusion = f32[64]{0:T(128)S(1)} fusion(bf16[64,32768]{1,0:T(8,128)(2,1)} %param.7, f32[32768]{0:T(1024)S(1)} %copy-done), kind=kLoop, calls=%fused_computation.3 | loop fusion | flops 6291392 | bytes 4325632 | tf_op jit(solution)/shard_map/reduce_sum | solution.py:24
  31.4 47.5 %all-to-all-done = bf16[128,2,64,128]{3,2,1,0:T(8,128)(2,1)} async-done(((bf16[128,2,64,128]{3,2,1,0:T(8,128)(2,1)}), bf16[128,2,64,128]{3,2,1,0:T(8,128)(2,1)}, u32[]{:S(2)}, u32[]{:S(2)}) %all-to-all-start) | async-done | bytes 4194336 | tf_op jit(solution)/shard_map/all_to_all | solution.py:28
  78.9 6.2 %gather_fusion.1 = bf16[384,64,128]{2,1,0:T(8,128)(2,1)} fusion(bf16[256,64,128]{2,1,0:T(8,128)(2,1)} %bitcast.1, s32[1024]{0:T(1024)S(1)} %pad_clamp_fusion), kind=kCustom, calls=%fused_computation.1 | custom fusion | bytes 12584448 | tf_op jit(solution)/shard_map/jit(_take)/gather | solution.py:30
  85.0 0.0 copy-start.3
  85.0 14.4 %fusion = f32[384,64,128]{2,1,0:T(8,128)} fusion(bf16[384,128,128]{2,1,0:T(8,128)(2,1)} %param.10, bf16[384,64,128]{2,1,0:T(8,128)(2,1)} %gather_fusion.1, pred[384]{0:T(512)(128)(4,1)S(1)} %compare_and_fusion), kind=kOutput, calls=%fused_computation.4 | convolution fusion | flops 808452096 | bytes 31457664 | tf_op jit(solution)/shard_map/pcs,pst->pct/dot_general | solution.py:31
  99.5 0.2 broadcast_in_dim.31
  99.7 0.0 copy-done.3
  99.7 0.0 copy-start.1
  99.7 39.5 %scatter_fusion = f32[64,64,128]{2,1,0:T(8,128)S(1)} fusion(f32[64,64,128]{2,1,0:T(8,128)S(1)} %broadcast_in_dim.31, s32[384]{0:T(512)S(1)} %copy-done.3, f32[384,64,128]{2,1,0:T(8,128)} %fusion), kind=kCustom, calls=%fused_computation.2 | custom fusion | flops 3145728 | bytes 37750272 | tf_op jit(solution)/shard_map/scatter-add | solution.py:32
  139.3 0.0 copy-done.1
  139.3 0.3 fusion.4
  139.6 9.9 %all-reduce.2 = (f32[64]{0:T(128)S(1)}, f32[64]{0:T(128)S(1)}) all-reduce(f32[64]{0:T(128)S(1)} %multiply_reduce_fusion, f32[64]{0:T(128)S(1)} %fusion.4), channel_id=1, replica_groups=mesh['row_0'=4,'row_1'=2,'col_0'=4,'col_1'=4] {'row_0'}, use_global_device_ids=true, to_apply=%region_2.3 | all-reduce | flops 128 | bytes 1024 | tf_op jit(solution)/shard_map/psum | solution.py:12
  149.5 2.5 %all-reduce.3 = (f32[64]{0:T(128)S(1)}, f32[64]{0:T(128)S(1)}) all-reduce(f32[64]{0:T(128)S(1)} %get-tuple-element.9, f32[64]{0:T(128)S(1)} %get-tuple-element.10), channel_id=1, replica_groups=mesh['row_0'=4,'row_1'=2,'col_0'=4,'col_1'=4] {'row_1'}, use_global_device_ids=true, to_apply=%region_3.4 | all-reduce | flops 128 | bytes 1024 | tf_op jit(solution)/shard_map/psum | solution.py:12
  151.9 8.4 %all-reduce.1 = (f32[64]{0:T(128)S(1)}, f32[64]{0:T(128)S(1)}) all-reduce(f32[64]{0:T(128)S(1)} %get-tuple-element.11, f32[64]{0:T(128)S(1)} %get-tuple-element.12), channel_id=1, replica_groups=mesh['row_0'=4,'row_1'=2,'col_0'=4,'col_1'=4] {'col_0'}, use_global_device_ids=true, to_apply=%region_4.5 | all-reduce | flops 128 | bytes 1024 | tf_op jit(solution)/shard_map/psum | solution.py:12
  160.3 9.7 %all-reduce = (f32[64]{0:T(128)S(1)}, f32[64]{0:T(128)S(1)}) all-reduce(f32[64]{0:T(128)S(1)} %get-tuple-element.7, f32[64]{0:T(128)S(1)} %get-tuple-element.8), channel_id=1, replica_groups=mesh['row_0'=4,'row_1'=2,'col_0'=4,'col_1'=4] {'col_1'}, use_global_device_ids=true, to_apply=%region_5.6 | all-reduce | flops 128 | bytes 1024 | tf_op jit(solution)/shard_map/psum | solution.py:12
  170.0 1.5 bitcast_multiply_fusion
  (5 shorter events, 0.0 us)
Async XLA Ops:
  16.5 11.7 %copy-start.2 = (s32[384]{0:T(512)S(1)}, s32[384]{0:T(512)}, u32[]{:S(2)}) copy-start(s32[384]{0:T(512)} %param.12) | copy-start | bytes 4612
  16.5 11.8 %copy-start = (f32[32768]{0:T(1024)S(1)}, f32[32768]{0:T(1024)}, u32[]{:S(2)}) copy-start(f32[32768]{0:T(1024)} %param.8) | copy-start | bytes 393220
  16.5 62.3 %all-to-all-start = ((bf16[128,2,64,128]{3,2,1,0:T(8,128)(2,1)}), bf16[128,2,64,128]{3,2,1,0:T(8,128)(2,1)}, u32[]{:S(2)}, u32[]{:S(2)}) async-start(bf16[128,2,64,128]{3,2,1,0:T(8,128)(2,1)} %bitcast.18), calls=%async_computation | async-start | bytes 8388608 | tf_op jit(solution)/shard_map/all_to_all | solution.py:28
  85.0 14.7 %copy-start.3 = (s32[384]{0:T(512)S(1)}, s32[384]{0:T(512)}, u32[]{:S(2)}) copy-start(s32[384]{0:T(512)} %param.13) | copy-start | bytes 4612
  99.7 39.5 %copy-start.1 = (f32[8192]{0:T(1024)S(1)}, f32[8192]{0:T(1024)}, u32[]{:S(2)}) copy-start(f32[8192]{0:T(1024)} %param.9) | copy-start | bytes 98308
where the time goes:
time: 173 us; the launch traced here: 172 us
  other arithmetic  49.8 us (29%)
  waiting for transfers between devices  47.5 us (27%)
  blocking collectives  30.5 us (18%)
  local copies, waits for them, and re-layouts  17.5 us (10%)
  matrix products  14.4 us (8%)
  starting transfers between devices  11.7 us (7%)
    all_to_all x1, waiting for transfers between devices, shards(): lax.all_to_all(outbound, ROW_COL, split_axis=0, concat_axis=0, tiled=True)  47.5 us
    scatter-add x1, other arithmetic, shards(): jax.ops.segment_sum(products, pair_target, num_segments=target_blocks)  39.5 us
    psum x4, blocking collectives, by_axis(): value = lax.psum(value, axis)  30.5 us
    dot_general x1, matrix products, shards(): jnp.einsum('pcs,pst->pct', picked, weights, preferred_element_type=jnp.fl...  14.4 us
    all_to_all x1, starting transfers between devices, shards(): lax.all_to_all(outbound, ROW_COL, split_axis=0, concat_axis=0, tiled=True)  11.7 us
    gather x1, local copies, waits for them, and re-layouts, shards(): picked = jnp.take(inbound, pair_slot, axis=0)  6.17 us
    reshape x1, local copies, waits for them, and re-layouts, shards(): blocks = src_field.reshape(columns, local_blocks, block_size)  5.32 us
    gather x1, local copies, waits for them, and re-layouts, shards(): outbound = jnp.take(blocks, chosen, axis=1)  5.25 us
  transfers between devices with their start and end apart: 1, of which 1 were waited for; matrix products, arithmetic and copies ran while one was open for 2% of the time, Pallas kernels for 0%

commit v1 on v0

v1 whole, which is shorter than its diff:
```python
import itertools
import random

import jax
import jax.numpy as jnp
from jax import lax
from jax.experimental import pallas as pl
from jax.experimental.pallas import tpu as pltpu
from jax.sharding import PartitionSpec as P

AXES = ("row", "col")
MESH = pl.DeviceIdType.MESH
PEERS = 128
CAP = 2
BLK = 128
VREG = 64
SB = 256
TB = 64
PAIRS = 384
CHUNKS = 8


def offsets_in_order():
    every = [o for o in itertools.product(range(4), range(4), range(4), range(2)) if any(o)]

    def canon(o):
        forms = [tuple((s * v) % 4 for v in o[p:3] + o[:p]) for p in range(3) for s in (1, -1)]
        return min(forms) + o[3:]

    sets = {}
    for o in every:
        sets.setdefault(canon(o), []).append(o)
    rng = random.Random(5)
    groups = list(sets.values())
    rng.shuffle(groups)
    for g in groups:
        rng.shuffle(g)
    flat = [o for g in groups for o in g]
    return sorted(flat, key=lambda o: sum(v != 0 for v in o))


ORDER = offsets_in_order()
NEAR = [o for o in ORDER if sum(v != 0 for v in o) == 1]
PLANE = [o for o in ORDER if o[2] == 0 and o[3] == 0]


def exchange_kernel(send_ref, src_hbm, inb, src, outb, load_sem, self_sem, ssem, rsem, round_sem):
    row, col = lax.axis_index("row"), lax.axis_index("col")
    me = row * 16 + col
    z, k, y, x = row // 2, lax.rem(row, 2), col // 4, lax.rem(col, 4)

    def peer(o):
        dx, dy, dz, dk = o
        r = lax.rem(z + dz, 4) * 2 + lax.rem(k + dk, 2)
        c = lax.rem(y + dy, 4) * 4 + lax.rem(x + dx, 4)
        return r, c

    def load(b):
        return pltpu.make_async_copy(src_hbm.at[:, pl.ds(pl.multiple_of(b * BLK, BLK), BLK)], src.at[b], load_sem)

    barrier = pltpu.get_barrier_semaphore()
    for o in NEAR:
        pl.semaphore_signal(barrier, inc=1, device_id=peer(o), device_id_type=MESH)

    @pl.loop(0, SB, unroll=8)
    def _(b):
        load(b).start()

    @pl.loop(0, SB, unroll=8)
    def _(b):
        load(b).wait()

    def stage(i, dest):
        for c in range(CAP):
            block = jnp.maximum(send_ref[c, dest], 0)
            outb[i, c] = src[block]

    copies = []

    def send(lo, hi):
        for i in range(lo, hi):
            r, c = peer(ORDER[i])
            cp = pltpu.make_async_remote_copy(
                src_ref=outb.at[i], dst_ref=inb.at[me], send_sem=ssem.at[i], recv_sem=rsem.at[i],
                device_id=(r, c), device_id_type=MESH)
            cp.start()
            copies.append(cp)

    def stage_all(lo, hi):
        for i in range(lo, hi):
            r, c = peer(ORDER[i])
            stage(i, r * 16 + c)

    stage_all(0, 10)
    pl.semaphore_wait(barrier, len(NEAR))
    for o in NEAR:
        pl.semaphore_signal(round_sem.at[0], inc=1, device_id=peer(o), device_id_type=MESH)
    send(0, 10)
    stage_all(10, 46)
    pl.semaphore_wait(round_sem.at[0], len(NEAR))
    for o in PLANE:
        pl.semaphore_signal(round_sem.at[1], inc=1, device_id=peer(o), device_id_type=MESH)
    send(10, 46)
    stage_all(46, 127)
    stage(127, me)
    own = pltpu.make_async_copy(outb.at[127], inb.at[me], self_sem)
    own.start()
    pl.semaphore_wait(round_sem.at[1], len(PLANE))
    send(46, 127)
    own.wait()
    for cp in copies:
        cp.wait_recv()
    for cp in copies:
        cp.wait_send()


def exchange(send_rows, src_field):
    return pl.pallas_call(
        exchange_kernel,
        out_shape=jax.ShapeDtypeStruct((PEERS, CAP, VREG, BLK), jnp.bfloat16),
        in_specs=[pl.BlockSpec(memory_space=pltpu.SMEM), pl.BlockSpec(memory_space=pl.ANY)],
        out_specs=pl.BlockSpec(memory_space=pl.ANY),
        scratch_shapes=[
            pltpu.VMEM((SB, VREG, BLK), jnp.bfloat16),
            pltpu.VMEM((PEERS, CAP, VREG, BLK), jnp.bfloat16),
            pltpu.SemaphoreType.DMA,
            pltpu.SemaphoreType.DMA,
            pltpu.SemaphoreType.DMA((PEERS,)),
            pltpu.SemaphoreType.DMA((PEERS,)),
            pltpu.SemaphoreType.REGULAR((2,)),
        ],
        compiler_params=pltpu.CompilerParams(
            collective_id=0, has_side_effects=True, vmem_limit_bytes=56 * 2**20),
        name="exchange",
    )(send_rows, src_field)


def regrid_kernel(slot_ref, target_ref, inb, weights, area_ref, out_ref, mass_ref, x, w, acc, xsem, wsem):
    load = pltpu.make_async_copy(inb, x, xsem)
    load.start()
    per = PAIRS // CHUNKS
    pieces = [pltpu.make_async_copy(weights.at[pl.ds(i * per, per)], w.at[pl.ds(i * per, per)], wsem.at[i])
              for i in range(CHUNKS)]
    for cp in pieces:
        cp.start()
    acc[...] = jnp.zeros_like(acc)
    load.wait()
    step = 8
    for i in range(CHUNKS):
        pieces[i].wait()

        @pl.loop(0, per // step)
        def _(j):
            base = i * per + j * step
            prods = []
            for u in range(step):
                prods.append(jnp.dot(x[slot_ref[base + u]], w[base + u], preferred_element_type=jnp.float32))
            for u in range(step):
                t = target_ref[base + u]
                acc[t] = acc[t] + prods[u]

    total = jnp.zeros((VREG, BLK), jnp.float32)
    for t in range(TB):
        v = acc[t]
        total = total + v * area_ref[pl.ds(t, 1), :]
        out_ref[:, t * BLK:(t + 1) * BLK] = v
    mass_ref[...] = total


def regrid(pair_slot, pair_target, inb, weights, tgt_area):
    smem = pl.BlockSpec(memory_space=pltpu.SMEM)
    vmem = pl.BlockSpec(memory_space=pltpu.VMEM)
    hbm = pl.BlockSpec(memory_space=pl.ANY)
    return pl.pallas_call(
        regrid_kernel,
        out_shape=[jax.ShapeDtypeStruct((VREG, TB * BLK), jnp.float32), jax.ShapeDtypeStruct((VREG, BLK), jnp.float32)],
        in_specs=[smem, smem, hbm, hbm, vmem],
        out_specs=[vmem, vmem],
        scratch_shapes=[
            pltpu.VMEM((PEERS * CAP, VREG, BLK), jnp.bfloat16),
            pltpu.VMEM((PAIRS, BLK, BLK), jnp.bfloat16),
            pltpu.VMEM((TB, VREG, BLK), jnp.float32),
            pltpu.SemaphoreType.DMA,
            pltpu.SemaphoreType.DMA((CHUNKS,)),
        ],
        compiler_params=pltpu.CompilerParams(vmem_limit_bytes=40 * 2**20),
        name="regrid",
    )(pair_slot, pair_target, inb, weights, tgt_area)


def shards(src_field, src_area, tgt_area, weights, send_index, pair_slot, pair_target):
    inb = exchange(send_index[0].T, src_field)
    source_local = jnp.sum(src_field.astype(jnp.float32) * src_area[None, :], axis=1)
    regridded, partial = regrid(pair_slot, pair_target, inb.reshape(PEERS * CAP, VREG, BLK), weights,
                                tgt_area.reshape(TB, BLK))
    masses = lax.psum(jnp.stack([source_local, jnp.sum(partial, axis=1)]), AXES)
    return regridded * (masses[0] / masses[1])[:, None]


def solution(mesh):
    placed = (P(None, AXES), P(AXES), P(AXES), P(AXES, None, None), P(AXES, None, None), P(AXES), P(AXES))
    return jax.shard_map(shards, mesh=mesh, in_specs=placed, out_specs=P(None, AXES), check_vma=False)
```

time: 173 us -> 145 us (0.84)
  the two profiles are of different devices: /device:TPU:0 before, /device:TPU:1 now
where the time goes in v1:
time: 145 us; the launch traced here: 144 us
  Pallas kernels  73.8 us (51%)
  blocking collectives  63.6 us (44%)
  other arithmetic  4.77 us (3%)
  local copies, waits for them, and re-layouts  2.2 us (2%)
    psum x1, blocking collectives, shards(): masses = lax.psum(jnp.stack([source_local, jnp.sum(partial, axis=1)]), AXES)  63.6 us
    pallas_call x1, Pallas kernels, exchange(): pl.pallas_call(exchange_kernel, out_shape=jax.ShapeDtypeStruct((PEERS, CA...  61.3 us
    pallas_call x1, Pallas kernels, regrid(): pl.pallas_call(regrid_kernel, out_shape=[jax.ShapeDtypeStruct((VREG, TB *...  12.6 us
    reduce_sum x1, other arithmetic, shards(): jnp.sum(src_field.astype(jnp.float32) * src_area[None, :], axis=1)  3.1 us

profile of v1, /device:TPU:1, one launch (start us, length us, event | category | flops | bytes accessed | tf_op | source)
XLA Modules:
  0.0 144.5 jit_solution(5637983929028897987)
XLA Ops:
  0.0 0.0 copy-start.1
  0.0 0.0 copy-start.2
  0.0 0.0 copy-start.3
  0.0 61.3 %exchange.1 = bf16[128,2,64,128]{3,2,1,0:T(8,128)(2,1)} custom-call(s32[2,128]{1,0:T(2,128)} %bitcast.13, bf16[64,32768]{1,0:T(8,128)(2,1)} %src_hbm.1), custom_call_target="tpu_custom_call" | custom-call | tf_op jit(solution)/shard_map/exchange/pallas_call | solution.py:118
  61.3 0.0 copy-done.1
  61.3 0.0 copy-done.2
  61.3 0.0 copy-done.3
  61.3 0.0 copy-start
  61.3 2.2 %copy-done = bf16[128,2,64,128]{3,2,1,0:T(8,128)(2,1)S(1)} copy-done((bf16[128,2,64,128]{3,2,1,0:T(8,128)(2,1)S(1)}, bf16[128,2,64,128]{3,2,1,0:T(8,128)(2,1)}, u32[]{:S(2)}) %copy-start) | copy-done | bytes 4194328
  63.5 0.0 copy-start.4
  63.5 12.6 %regrid.1 = (f32[64,8192]{1,0:T(8,128)S(1)}, f32[64,128]{1,0:T(8,128)S(1)}) custom-call(s32[384]{0:T(512)S(1)} %copy-done.2, s32[384]{0:T(512)S(1)} %copy-done.3, bf16[256,64,128]{2,1,0:T(8,128)(2,1)S(1)} %bitcast.9, bf16[384,128,128]{2,1,0:T(8,128)(2,1)} %weights.1, f32[64,128]{1,0:T(8,128)S(1)} %bitcast.10), custom_call_target="tpu_custom_call" | custom-call | tf_op jit(solution)/shard_map/regrid/pallas_call | solution.py:174
  76.1 0.1 reduce_sum.19
  76.2 0.0 copy-done.4
  76.2 3.1 %multiply_reduce_fusion = f32[64]{0:T(128)S(1)} fusion(bf16[64,32768]{1,0:T(8,128)(2,1)} %src_hbm.1, f32[32768]{0:T(1024)S(1)} %copy-done.4), kind=kLoop, calls=%fused_computation | loop fusion | flops 6291392 | bytes 4325632 | tf_op jit(solution)/shard_map/reduce_sum | solution.py:193
  79.3 63.6 %psum.7 = f32[2,64]{1,0:T(2,128)S(1)} all-reduce(f32[2,64]{1,0:T(2,128)S(1)} %pad_maximum_fusion), channel_id=1, replica_groups=mesh['row'=8,'col'=16] {'row','col'}, use_global_device_ids=true, to_apply=%region_2.0 | all-reduce | flops 128 | bytes 1024 | tf_op jit(solution)/shard_map/psum | solution.py:196
  142.9 1.6 %broadcast_multiply_fusion = f32[64,8192]{1,0:T(8,128)} fusion(f32[64,8192]{1,0:T(8,128)S(1)} %get-tuple-element.7, f32[64]{0:T(128)S(1)} %fusion), kind=kLoop, calls=%fused_computation.1 | loop fusion | flops 524288 | bytes 4194560 | tf_op jit(solution)/shard_map/mul | solution.py:197
  (2 shorter events, 0.0 us)
Async XLA Ops:
  0.0 61.3 %copy-start.1 = (f32[8192]{0:T(1024)S(1)}, f32[8192]{0:T(1024)}, u32[]{:S(2)}) copy-start(f32[8192]{0:T(1024)} %param.9) | copy-start | bytes 98308
  0.0 61.3 %copy-start.2 = (s32[384]{0:T(512)S(1)}, s32[384]{0:T(512)}, u32[]{:S(2)}) copy-start(s32[384]{0:T(512)} %slot_ref.1) | copy-start | bytes 4612
  0.0 61.3 %copy-start.3 = (s32[384]{0:T(512)S(1)}, s32[384]{0:T(512)}, u32[]{:S(2)}) copy-start(s32[384]{0:T(512)} %target_ref.1) | copy-start | bytes 4612
  61.3 2.2 %copy-start = (bf16[128,2,64,128]{3,2,1,0:T(8,128)(2,1)S(1)}, bf16[128,2,64,128]{3,2,1,0:T(8,128)(2,1)}, u32[]{:S(2)}) copy-start(bf16[128,2,64,128]{3,2,1,0:T(8,128)(2,1)} %exchange.1) | copy-start | bytes 12582916
  63.5 12.7 %copy-start.4 = (f32[32768]{0:T(1024)S(1)}, f32[32768]{0:T(1024)}, u32[]{:S(2)}) copy-start(f32[32768]{0:T(1024)} %param.8) | copy-start | bytes 393220

commit v2 on v1

--- a/solution.py
+++ b/solution.py
@@ -44,7 +44,22 @@
 PLANE = [o for o in ORDER if o[2] == 0 and o[3] == 0]
 
 
-def exchange_kernel(send_ref, src_hbm, inb, src, outb, load_sem, self_sem, ssem, rsem, round_sem):
+INDEX = {o: i for i, o in enumerate(ORDER)}
+OPPOSITE = [INDEX[tuple((4 - v) % 4 for v in o[:3]) + o[3:]] for o in ORDER]
+OTHERS = PEERS - 1
+FIRST, SECOND = 80, 112
+
+
+def split3(v):
+    hi = v.astype(jnp.bfloat16)
+    rest = v - hi.astype(jnp.float32)
+    mid = rest.astype(jnp.bfloat16)
+    return hi, mid, (rest - mid.astype(jnp.float32)).astype(jnp.bfloat16)
+
+
+def exchange_kernel(send_ref, target_ref, slot_ref, src_area_ref, tgt_area_ref, src_hbm, weights, inb, ratio_ref,
+                    src, outb, w, area3, upair, uout, uin, mout, min_, load_sem, self_sem, wsem, ssem, rsem,
+                    usend, urecv, msend, mrecv, round_sem):
     row, col = lax.axis_index("row"), lax.axis_index("col")
     me = row * 16 + col
     z, k, y, x = row // 2, lax.rem(row, 2), col // 4, lax.rem(col, 4)
@@ -65,6 +80,20 @@
     @pl.loop(0, SB, unroll=8)
     def _(b):
         load(b).start()
+
+    per = PAIRS // CHUNKS
+    pieces = [pltpu.make_async_copy(weights.at[pl.ds(i * per, per)], w.at[pl.ds(i * per, per)], wsem.at[i])
+              for i in range(CHUNKS)]
+    for cp in pieces:
+        cp.start()
+
+    rows = lax.broadcasted_iota(jnp.int32, (16, BLK), 0)
+
+    @pl.loop(0, TB)
+    def _(t):
+        hi, mid, lo = (p.astype(jnp.float32) for p in split3(tgt_area_ref[pl.ds(t, 1), :]))
+        stacked = jnp.where(rows == 0, hi, jnp.where(rows == 1, mid, jnp.where(rows == 2, lo, 0.0)))
+        area3[t] = stacked.astype(jnp.bfloat16)
 
     @pl.loop(0, SB, unroll=8)
     def _(b):
@@ -101,41 +130,106 @@
     for o in PLANE:
         pl.semaphore_signal(round_sem.at[1], inc=1, device_id=peer(o), device_id_type=MESH)
     send(10, 46)
-    stage_all(46, 127)
-    stage(127, me)
-    own = pltpu.make_async_copy(outb.at[127], inb.at[me], self_sem)
+    stage_all(46, OTHERS)
+    stage(OTHERS, me)
+    own = pltpu.make_async_copy(outb.at[OTHERS], inb.at[me], self_sem)
     own.start()
     pl.semaphore_wait(round_sem.at[1], len(PLANE))
-    send(46, 127)
+    send(46, FIRST)
+
+    step = 8
+    for i in range(CHUNKS):
+        pieces[i].wait()
+
+        @pl.loop(0, per // step)
+        def _(j):
+            base = i * per + j * step
+            sums = []
+            for u in range(step):
+                r = lax.dot_general(area3[target_ref[base + u]], w[base + u], (((1,), (1,)), ((), ())),
+                                    preferred_element_type=jnp.float32)
+                sums.append(jnp.sum(r[0:8], axis=0, keepdims=True))
+            upair[pl.ds(pl.multiple_of(base, step), step), :] = jnp.concatenate(sums, axis=0)
+
+    parts = split3(upair[...])
+    which = lax.broadcasted_iota(jnp.int32, (PEERS, PAIRS), 0) * CAP
+    for c in range(CAP):
+        chosen = jnp.where(slot_ref[...] == which + c, 1.0, 0.0).astype(jnp.bfloat16)
+        total = sum(jnp.dot(chosen, p, preferred_element_type=jnp.float32) for p in parts)
+        for d in range(PEERS):
+            uout[d, :, c * BLK:(c + 1) * BLK] = total[d:d + 1, :]
+
+    def source_mass(b, total):
+        return total + src[b].astype(jnp.float32) * src_area_ref[pl.ds(b, 1), :]
+
+    mass_s = lax.fori_loop(0, SB, source_mass, jnp.zeros((VREG, BLK), jnp.float32), unroll=4)
+
+    for i in range(OTHERS):
+        r, c = peer(ORDER[i])
+        pltpu.make_async_remote_copy(
+            src_ref=uout.at[r * 16 + c], dst_ref=uin.at[OPPOSITE[i]], send_sem=usend, recv_sem=urecv,
+            device_id=(r, c), device_id_type=MESH).start()
+    send(FIRST, SECOND)
+
+    def weighed(blocks, u, total):
+        for c in range(CAP):
+            total = total + blocks[c].astype(jnp.float32) * u[:, c * BLK:(c + 1) * BLK]
+        return total
+
+    mass_t = weighed(outb.at[OTHERS], uout[me], jnp.zeros((VREG, BLK), jnp.float32))
+    pltpu.make_async_copy(uin, uin, urecv).wait()
+    mass_t = lax.fori_loop(0, OTHERS, lambda i, total: weighed(outb.at[i], uin[i], total), mass_t)
+    local = jnp.sum(jnp.concatenate([mass_s, mass_t], axis=0).T, axis=0, keepdims=True)
+    mout[...] = local
+    send(SECOND, SECOND + 4)
+    for i in range(OTHERS):
+        pltpu.make_async_remote_copy(
+            src_ref=mout, dst_ref=min_.at[i], send_sem=msend, recv_sem=mrecv,
+            device_id=peer(ORDER[i]), device_id_type=MESH).start()
+    send(SECOND + 4, OTHERS)
+    pltpu.make_async_copy(min_, min_, mrecv).wait()
+    total = lax.fori_loop(0, OTHERS, lambda i, t: t + min_[i], local)
+    ratio_ref[...] = total / pltpu.roll(total, VREG, 1)
     own.wait()
     for cp in copies:
         cp.wait_recv()
     for cp in copies:
         cp.wait_send()
-
-
-def exchange(send_rows, src_field):
+    pltpu.make_async_copy(uin, uin, usend).wait()
+    pltpu.make_async_copy(min_, min_, msend).wait()
+
+
+def exchange(send_rows, pair_target, pair_slot, src_area, tgt_area, src_field, weights):
+    smem = pl.BlockSpec(memory_space=pltpu.SMEM)
+    vmem = pl.BlockSpec(memory_space=pltpu.VMEM)
+    hbm = pl.BlockSpec(memory_space=pl.ANY)
+    dma = pltpu.SemaphoreType.DMA
     return pl.pallas_call(
         exchange_kernel,
-        out_shape=jax.ShapeDtypeStruct((PEERS, CAP, VREG, BLK), jnp.bfloat16),
-        in_specs=[pl.BlockSpec(memory_space=pltpu.SMEM), pl.BlockSpec(memory_space=pl.ANY)],
-        out_specs=pl.BlockSpec(memory_space=pl.ANY),
+        out_shape=[jax.ShapeDtypeStruct((PEERS, CAP, VREG, BLK), jnp.bfloat16),
+                   jax.ShapeDtypeStruct((1, BLK), jnp.float32)],
+        in_specs=[smem, smem, vmem, vmem, vmem, hbm, hbm],
+        out_specs=[hbm, vmem],
         scratch_shapes=[
             pltpu.VMEM((SB, VREG, BLK), jnp.bfloat16),
             pltpu.VMEM((PEERS, CAP, VREG, BLK), jnp.bfloat16),
-            pltpu.SemaphoreType.DMA,
-            pltpu.SemaphoreType.DMA,
-            pltpu.SemaphoreType.DMA((PEERS,)),
-            pltpu.SemaphoreType.DMA((PEERS,)),
+            pltpu.VMEM((PAIRS, BLK, BLK), jnp.bfloat16),
+            pltpu.VMEM((TB, 16, BLK), jnp.bfloat16),
+            pltpu.VMEM((PAIRS, BLK), jnp.float32),
+            pltpu.VMEM((PEERS, 1, CAP * BLK), jnp.float32),
+            pltpu.VMEM((OTHERS, 1, CAP * BLK), jnp.float32),
+            pltpu.VMEM((1, BLK), jnp.float32),
+            pltpu.VMEM((OTHERS, 1, BLK), jnp.float32),
+            dma, dma, dma((CHUNKS,)), dma((PEERS,)), dma((PEERS,)), dma, dma, dma, dma,
             pltpu.SemaphoreType.REGULAR((2,)),
         ],
         compiler_params=pltpu.CompilerParams(
-            collective_id=0, has_side_effects=True, vmem_limit_bytes=56 * 2**20),
+            collective_id=0, has_side_effects=True, vmem_limit_bytes=60 * 2**20),
         name="exchange",
-    )(send_rows, src_field)
-
-
-def regrid_kernel(slot_ref, target_ref, inb, weights, area_ref, out_ref, mass_ref, x, w, acc, xsem, wsem):
+    )(send_rows, pair_target, pair_slot, src_area, tgt_area, src_field, weights)
+
+
+def regrid_kernel(slot_ref, target_ref, inb, weights, ratio_ref, out_ref, x, w, acc, xsem, wsem):
     load = pltpu.make_async_copy(inb, x, xsem)
     load.start()
     per = PAIRS // CHUNKS
@@ -159,23 +253,20 @@
                 t = target_ref[base + u]
                 acc[t] = acc[t] + prods[u]
 
-    total = jnp.zeros((VREG, BLK), jnp.float32)
+    ratio = jnp.broadcast_to(ratio_ref[...], (BLK, BLK)).T[:VREG]
     for t in range(TB):
-        v = acc[t]
-        total = total + v * area_ref[pl.ds(t, 1), :]
-        out_ref[:, t * BLK:(t + 1) * BLK] = v
-    mass_ref[...] = total
-
-
-def regrid(pair_slot, pair_target, inb, weights, tgt_area):
+        out_ref[:, t * BLK:(t + 1) * BLK] = acc[t] * ratio
+
+
+def regrid(pair_slot, pair_target, inb, weights, ratio):
     smem = pl.BlockSpec(memory_space=pltpu.SMEM)
     vmem = pl.BlockSpec(memory_space=pltpu.VMEM)
     hbm = pl.BlockSpec(memory_space=pl.ANY)
     return pl.pallas_call(
         regrid_kernel,
-        out_shape=[jax.ShapeDtypeStruct((VREG, TB * BLK), jnp.float32), jax.ShapeDtypeStruct((VREG, BLK), jnp.float32)],
+        out_shape=jax.ShapeDtypeStruct((VREG, TB * BLK), jnp.float32),
         in_specs=[smem, smem, hbm, hbm, vmem],
-        out_specs=[vmem, vmem],
+        out_specs=vmem,
         scratch_shapes=[
             pltpu.VMEM((PEERS * CAP, VREG, BLK), jnp.bfloat16),
             pltpu.VMEM((PAIRS, BLK, BLK), jnp.bfloat16),
@@ -183,18 +274,15 @@
             pltpu.SemaphoreType.DMA,
             pltpu.SemaphoreType.DMA((CHUNKS,)),
         ],
-        compiler_params=pltpu.CompilerParams(vmem_limit_bytes=40 * 2**20),
+        compiler_params=pltpu.CompilerParams(vmem_limit_bytes=60 * 2**20),
         name="regrid",
-    )(pair_slot, pair_target, inb, weights, tgt_area)
+    )(pair_slot, pair_target, inb, weights, ratio)
 
 
 def shards(src_field, src_area, tgt_area, weights, send_index, pair_slot, pair_target):
-    inb = exchange(send_index[0].T, src_field)
-    source_local = jnp.sum(src_field.astype(jnp.float32) * src_area[None, :], axis=1)
-    regridded, partial = regrid(pair_slot, pair_target, inb.reshape(PEERS * CAP, VREG, BLK), weights,
-                                tgt_area.reshape(TB, BLK))
-    masses = lax.psum(jnp.stack([source_local, jnp.sum(partial, axis=1)]), AXES)
-    return regridded * (masses[0] / masses[1])[:, None]
+    inb, ratio = exchange(send_index[0].T, pair_target, pair_slot.reshape(1, PAIRS), src_area.reshape(SB, BLK),
+                          tgt_area.reshape(TB, BLK), src_field, weights)
+    return regrid(pair_slot, pair_target, inb.reshape(PEERS * CAP, VREG, BLK), weights, ratio)
 
 
 def solution(mesh):

time: 145 us -> 84.1 us (0.58)
  blocking collectives: 63.6 us -> 0 us
  Pallas kernels: 73.8 us -> 82.7 us
  other arithmetic: 4.77 us -> 0 us
    psum x1 -> x0, blocking collectives: 63.6 us -> none  [shards(): masses = lax.psum(jnp.stack([source_local, jnp.sum(partial, axis=1)]), AXES)]
    pallas_call x2, Pallas kernels: 73.8 us -> 82.7 us  [the longest x1 64.9 us: exchange(): pl.pallas_call(exchange_kernel, out_shape=[jax.ShapeDtypeStruct((PEERS, C...]
    reduce_sum x2 -> x0, other arithmetic: 3.21 us -> none  [the longest x1 3.1 us: shards(): jnp.sum(src_field.astype(jnp.float32) * src_area[None, :], axis=1)]
    unnamed x10 -> x0, local copies, waits for them, and re-layouts: 2.2 us -> none
    mul x1 -> x0, other arithmetic: 1.55 us -> none  [shards(): return regridded * (masses[0] / masses[1])[:, None]]
where the time goes in v2:
time: 84.1 us; the launch traced here: 84 us
  Pallas kernels  82.7 us (98%)
  local copies, waits for them, and re-layouts  1.24 us (1%)
    pallas_call x1, Pallas kernels, exchange(): pl.pallas_call(exchange_kernel, out_shape=[jax.ShapeDtypeStruct((PEERS, C...  64.9 us
    pallas_call x1, Pallas kernels, regrid(): pl.pallas_call(regrid_kernel, out_shape=jax.ShapeDtypeStruct((VREG, TB *...  17.8 us

profile of v2, /device:TPU:1, one launch (start us, length us, event | category | flops | bytes accessed | tf_op | source)
XLA Modules:
  0.0 84.0 jit_solution(5165199572391941130)
XLA Ops:
  0.0 1.2 %reshape.12.slot_ref = s32[1,384]{1,0:T(1,128)} reshape(s32[384]{0:T(512)} %slot_ref.1) | data formatting | bytes 3072 | tf_op jit(solution)/shard_map/reshape | solution.py:283
  1.2 64.9 %exchange.1 = (bf16[128,2,64,128]{3,2,1,0:T(8,128)(2,1)}, f32[1,128]{1,0:T(1,128)}) custom-call(s32[2,128]{1,0:T(2,128)} %bitcast.9, s32[384]{0:T(512)} %target_ref.3, s32[1,384]{1,0:T(1,128)} %reshape.12.slot_ref, f32[256,128]{1,0:T(8,128)} %bitcast.7, f32[64,128]{1,0:T(8,128)} %bitcast.8, bf16[64,32768]{1,0:T(8,128)(2,1)} %src_hbm.1, ...), custom_call_target="tpu_custom_call" | custom-call | tf_op jit(solution)/shard_map/exchange/pallas_call | solution.py:207
  66.2 17.8 %regrid.1 = f32[64,8192]{1,0:T(8,128)} custom-call(s32[384]{0:T(512)} %slot_ref.1, s32[384]{0:T(512)} %target_ref.3, bf16[256,64,128]{2,1,0:T(8,128)(2,1)} %bitcast.6, bf16[384,128,128]{2,1,0:T(8,128)(2,1)} %weights.3, f32[1,128]{1,0:T(1,128)} %get-tuple-element.8.ratio_ref), custom_call_target="tpu_custom_call" | custom-call | tf_op jit(solution)/shard_map/regrid/pallas_call | solution.py:265

commit v3 on v2

v3 whole, which is shorter than its diff:
```python
import itertools
import random

import jax
import jax.numpy as jnp
from jax import lax
from jax.experimental import pallas as pl
from jax.experimental.pallas import tpu as pltpu
from jax.sharding import PartitionSpec as P

AXES = ("row", "col")
MESH = pl.DeviceIdType.MESH
PEERS = 128
CAP = 2
BLK = 128
VREG = 64
SB = 256
TB = 64
PAIRS = 384
CHUNKS = 8


def offsets_in_order():
    every = [o for o in itertools.product(range(4), range(4), range(4), range(2)) if any(o)]

    def canon(o):
        forms = [tuple((s * v) % 4 for v in o[p:3] + o[:p]) for p in range(3) for s in (1, -1)]
        return min(forms) + o[3:]

    sets = {}
    for o in every:
        sets.setdefault(canon(o), []).append(o)
    rng = random.Random(5)
    groups = list(sets.values())
    rng.shuffle(groups)
    for g in groups:
        rng.shuffle(g)
    flat = [o for g in groups for o in g]
    return sorted(flat, key=lambda o: (sum(v != 0 for v in o), group_of(o)))


def group_of(o):
    differing = sum(v != 0 for v in o)
    if differing <= 2:
        return 0
    if differing == 3:
        return 1 + o[3]
    return 3 if sum(o[:3]) % 3 else 4


ORDER = offsets_in_order()
GROUPS = 5
ENDS = [sum(group_of(o) <= g for o in ORDER) for g in range(GROUPS)]
FIRST = 90
ROOM = (160, 96, 96, 80)
NEAR = [o for o in ORDER if sum(v != 0 for v in o) == 1]
PLANE = [o for o in ORDER if o[2] == 0 and o[3] == 0]


INDEX = {o: i for i, o in enumerate(ORDER)}
OPPOSITE = [INDEX[tuple((4 - v) % 4 for v in o[:3]) + o[3:]] for o in ORDER]
OTHERS = PEERS - 1
PER = PAIRS // CHUNKS


def split3(v):
    hi = v.astype(jnp.bfloat16)
    rest = v - hi.astype(jnp.float32)
    mid = rest.astype(jnp.bfloat16)
    return hi, mid, (rest - mid.astype(jnp.float32)).astype(jnp.bfloat16)


def columns(row):
    parts = [jnp.broadcast_to(row[:, c:c + BLK], (BLK, BLK)).T for c in range(0, PAIRS, BLK)]
    return jnp.concatenate(parts, axis=0)


def add_rows(m):
    acc = m[0:8]
    for i in range(8, PAIRS, 8):
        acc = acc + m[i:i + 8]
    for shift in (4, 2, 1):
        acc = acc + pltpu.roll(acc, shift, 0)
    return acc[0:1]


def pair_table(slot, target, z, k, y, x):
    sender = lax.shift_right_logical(slot, 1)
    dz = (z - lax.shift_right_logical(sender, 5) + 4) & 3
    dk = (k - lax.shift_right_logical(sender, 4)) & 1
    dy = (y - lax.shift_right_logical(sender, 2)) & 3
    dx = (x - sender) & 3
    differing = sum(jnp.where(v != 0, 1, 0) for v in (dx, dy, dz, dk))
    steps = dx + dy + dz
    last = jnp.where((steps == 3) | (steps == 6) | (steps == 9), 4, 3)
    group = jnp.where(differing <= 2, 0, jnp.where(differing == 3, 1 + dk, last))
    lane = lax.broadcasted_iota(jnp.int32, (1, PAIRS), 1)
    key = (group * TB + target) * 512 + lane
    key_col = columns(key)
    rank = jnp.concatenate([add_rows(jnp.where(key_col < key[:, c:c + BLK], 1, 0)) for c in range(0, PAIRS, BLK)], axis=1)
    packed_col = columns(lane * 16384 + slot * 64 + target)
    rank_col = columns(rank)
    lanes = lax.broadcasted_iota(jnp.int32, (PAIRS, BLK), 1)
    packed = [add_rows(jnp.where(rank_col == lanes + c, packed_col, 0)) for c in range(0, PAIRS, BLK)]
    upto = [add_rows(jnp.where(key_col < (lanes + (c + 1)) * 512, 1, 0)) for c in range(0, PAIRS, BLK)]
    return jnp.concatenate(packed, axis=1), jnp.concatenate(upto, axis=1)


def exchange_kernel(send_ref, target_ref, slots_ref, targets_ref, src_area_ref, tgt_area_ref, src_hbm, weights,
                    inb, partial, table_ref, ratio_ref,
                    src, outb, w, xa, xb, prods, acc, area3, upair, uout, uin, mout, min_, table,
                    load_sem, self_sem, wsem, ssem, rsem, usend, urecv, msend, mrecv, tsem, xsem, psem, round_sem):
    row, col = lax.axis_index("row"), lax.axis_index("col")
    me = row * 16 + col
    z, k, y, x_ = row // 2, lax.rem(row, 2), col // 4, lax.rem(col, 4)

    def peer(o, sign=1):
        dx, dy, dz, dk = o
        r = lax.rem(z + sign * dz + 4, 4) * 2 + lax.rem(k + dk, 2)
        c = lax.rem(y + sign * dy + 4, 4) * 4 + lax.rem(x_ + sign * dx + 4, 4)
        return r, c

    def load(b):
        return pltpu.make_async_copy(src_hbm.at[:, pl.ds(pl.multiple_of(b * BLK, BLK), BLK)], src.at[b], load_sem)

    xs = (xa, xb)
    barrier = pltpu.get_barrier_semaphore()
    for o in NEAR:
        pl.semaphore_signal(barrier, inc=1, device_id=peer(o), device_id_type=MESH)
    pieces = [pltpu.make_async_copy(weights.at[pl.ds(i * PER, PER)], w.at[pl.ds(i * PER, PER)], wsem.at[i])
              for i in range(CHUNKS)]

    @pl.loop(0, SB, unroll=8)
    def _(b):
        load(b).start()

    step = 16

    def weight_sums(i):
        pieces[i].wait()

        @pl.loop(0, PER // step)
        def _(j):
            base = i * PER + j * step
            sums = []
            for u in range(step):
                r = lax.dot_general(area3[target_ref[base + u]], w[base + u], (((1,), (1,)), ((), ())),
                                    preferred_element_type=jnp.float32)
                sums.append(jnp.sum(r[0:8], axis=0, keepdims=True))
            upair[pl.ds(pl.multiple_of(base, step), step), :] = jnp.concatenate(sums, axis=0)

    def stage(lo, hi):
        for i in range(lo, hi):
            if i < OTHERS:
                r, c = peer(ORDER[i])
                dest = r * 16 + c
            else:
                dest = me
            for c in range(CAP):
                outb[i, c] = src[jnp.maximum(send_ref[c, dest], 0)]

    copies = []

    def send(lo, hi):
        for i in range(lo, hi):
            r, c = peer(ORDER[i])
            cp = pltpu.make_async_remote_copy(
                src_ref=outb.at[i], dst_ref=inb.at[me], send_sem=ssem.at[i], recv_sem=rsem.at[i],
                device_id=(r, c), device_id_type=MESH)
            cp.start()
            copies.append(cp)

    def fetch(g, with_own=False):
        lo, hi, x = ENDS[g - 1] if g else 0, ENDS[g], xs[g % 2]
        local = []
        for i in range(lo, hi):
            copies[i].wait_recv()
            r, c = peer(ORDER[i], -1)
            s = r * 16 + c
            local.append(pltpu.make_async_copy(inb.at[s], x.at[pl.ds(s * CAP, CAP)], xsem.at[i]))
            local[-1].start()
        if with_own:
            own.wait()
            local.append(pltpu.make_async_copy(inb.at[me], x.at[pl.ds(me * CAP, CAP)], xsem.at[OTHERS]))
            local[-1].start()
        return local

    def regrid_group(g, local):
        room, x = ROOM[g], xs[g % 2]
        for cp in local:
            cp.wait()
        start = table[1, g * TB - 1] if g else 0

        def some(n, carry):
            total, before = carry
            for u in range(step):
                entry = table[0, jnp.minimum(start + n * step + u, PAIRS - 1)]
                t = entry & 63
                product = jnp.dot(x[lax.shift_right_logical(entry, 6) & 255], w[lax.shift_right_logical(entry, 14)],
                                  preferred_element_type=jnp.float32)
                total = total * jnp.where(t == before, 1.0, 0.0) + product
                before = t
                prods[n * step + u] = total
            return total, before

        lax.fori_loop(0, room // step, some, (jnp.zeros((VREG, BLK), jnp.float32), jnp.int32(-1)))

        @pl.loop(0, TB)
        def _(t):
            end = table[1, g * TB + t]
            begin = table[1, jnp.maximum(g * TB + t - 1, 0)]
            if g == 0:
                begin = jnp.where(t == 0, 0, begin)
            there = (end > begin) & (begin - start < room)
            v = prods[jnp.clip(end - 1 - start, 0, room - 1)]
            v = jnp.where(there, v, 0.0)
            acc[t] = v if g == 0 else acc[t] + v


    @pl.loop(0, SB, unroll=8)
    def _(b):
        load(b).wait()

    for cp in pieces:
        cp.start()
    stage(0, 10)
    pl.semaphore_wait(barrier, len(NEAR))
    for o in NEAR:
        pl.semaphore_signal(round_sem.at[0], inc=1, device_id=peer(o), device_id_type=MESH)
    send(0, 10)
    stage(10, 46)
    rows = lax.broadcasted_iota(jnp.int32, (16, BLK), 0)

    @pl.loop(0, TB)
    def _(t):
        hi, mid, lo = (p.astype(jnp.float32) for p in split3(tgt_area_ref[pl.ds(t, 1), :]))
        stacked = jnp.where(rows == 0, hi, jnp.where(rows == 1, mid, jnp.where(rows == 2, lo, 0.0)))
        area3[t] = stacked.astype(jnp.bfloat16)

    weight_sums(0)
    pl.semaphore_wait(round_sem.at[0], len(NEAR))
    for o in PLANE:
        pl.semaphore_signal(round_sem.at[1], inc=1, device_id=peer(o), device_id_type=MESH)
    send(10, 46)
    stage(46, PEERS)
    own = pltpu.make_async_copy(outb.at[OTHERS], inb.at[me], self_sem)
    own.start()
    weight_sums(1)
    weight_sums(2)
    pl.semaphore_wait(round_sem.at[1], len(PLANE))
    send(46, FIRST)
    for i in range(3, 8):
        weight_sums(i)

    parts = split3(upair[...])
    slots = slots_ref[...].reshape(1, PAIRS)
    which = lax.broadcasted_iota(jnp.int32, (PEERS, PAIRS), 0) * CAP
    for c in range(CAP):
        chosen = jnp.where(slots == which + c, 1.0, 0.0).astype(jnp.bfloat16)
        total = sum(jnp.dot(chosen, p, preferred_element_type=jnp.float32) for p in parts)
        for d in range(PEERS):
            uout[d, :, c * BLK:(c + 1) * BLK] = total[d:d + 1, :]

    for i in range(OTHERS):
        r, c = peer(ORDER[i])
        pltpu.make_async_remote_copy(
            src_ref=uout.at[r * 16 + c], dst_ref=uin.at[OPPOSITE[i]], send_sem=usend, recv_sem=urecv,
            device_id=(r, c), device_id_type=MESH).start()
    send(FIRST, OTHERS)
    packed, upto = pair_table(slots, targets_ref[...].reshape(1, PAIRS), z, k, y, x_)
    table_ref[0:1, :] = packed
    table_ref[1:2, :] = upto

    def source_mass(b, total):
        return total + src[b].astype(jnp.float32) * src_area_ref[pl.ds(b, 1), :]

    scalars = pltpu.make_async_copy(table_ref, table, tsem)
    scalars.start()
    local = fetch(0, with_own=True)
    mass_s = lax.fori_loop(0, SB, source_mass, jnp.zeros((VREG, BLK), jnp.float32), unroll=4)
    scalars.wait()
    regrid_group(0, local)
    local = fetch(1)

    def weighed(blocks, u, total):
        for c in range(CAP):
            total = total + blocks[c].astype(jnp.float32) * u[:, c * BLK:(c + 1) * BLK]
        return total

    mass_t = weighed(outb.at[OTHERS], uout[me], jnp.zeros((VREG, BLK), jnp.float32))
    pltpu.make_async_copy(uin, uin, urecv).wait()
    mass_t = lax.fori_loop(0, OTHERS, lambda i, total: weighed(outb.at[i], uin[i], total), mass_t)
    sums = jnp.sum(jnp.concatenate([mass_s, mass_t], axis=0).T, axis=0, keepdims=True)
    mout[...] = sums
    for i in range(OTHERS):
        pltpu.make_async_remote_copy(
            src_ref=mout, dst_ref=min_.at[i], send_sem=msend, recv_sem=mrecv,
            device_id=peer(ORDER[i]), device_id_type=MESH).start()
    for g in range(1, GROUPS - 1):
        regrid_group(g, local)
        if g < GROUPS - 2:
            local = fetch(g + 1)
    out = pltpu.make_async_copy(acc, partial, psem)
    out.start()
    pltpu.make_async_copy(min_, min_, mrecv).wait()
    total = lax.fori_loop(0, OTHERS, lambda i, t: t + min_[i], sums)
    ratio_ref[...] = total / pltpu.roll(total, VREG, 1)
    for i in range(ENDS[3], OTHERS):
        copies[i].wait_recv()
    for cp in copies:
        cp.wait_send()
    pltpu.make_async_copy(uin, uin, usend).wait()
    pltpu.make_async_copy(min_, min_, msend).wait()
    out.wait()


def exchange(send_rows, pair_target, pair_slot, src_area, tgt_area, src_field, weights):
    smem = pl.BlockSpec(memory_space=pltpu.SMEM)
    vmem = pl.BlockSpec(memory_space=pltpu.VMEM)
    hbm = pl.BlockSpec(memory_space=pl.ANY)
    dma = pltpu.SemaphoreType.DMA
    return pl.pallas_call(
        exchange_kernel,
        out_shape=[jax.ShapeDtypeStruct((PEERS, CAP, VREG, BLK), jnp.bfloat16),
                   jax.ShapeDtypeStruct((TB, VREG, BLK), jnp.float32),
                   jax.ShapeDtypeStruct((8, PAIRS), jnp.int32),
                   jax.ShapeDtypeStruct((1, BLK), jnp.float32)],
        in_specs=[smem, smem, vmem, vmem, vmem, vmem, hbm, hbm],
        out_specs=[hbm, hbm, vmem, vmem],
        scratch_shapes=[
            pltpu.VMEM((SB, VREG, BLK), jnp.bfloat16),
            pltpu.VMEM((PEERS, CAP, VREG, BLK), jnp.bfloat16),
            pltpu.VMEM((PAIRS, BLK, BLK), jnp.bfloat16),
            pltpu.VMEM((PEERS * CAP, VREG, BLK), jnp.bfloat16),
            pltpu.VMEM((PEERS * CAP, VREG, BLK), jnp.bfloat16),
            pltpu.VMEM((max(ROOM), VREG, BLK), jnp.float32),
            pltpu.VMEM((TB, VREG, BLK), jnp.float32),
            pltpu.VMEM((TB, 16, BLK), jnp.bfloat16),
            pltpu.VMEM((PAIRS, BLK), jnp.float32),
            pltpu.VMEM((PEERS, 1, CAP * BLK), jnp.float32),
            pltpu.VMEM((OTHERS, 1, CAP * BLK), jnp.float32),
            pltpu.VMEM((1, BLK), jnp.float32),
            pltpu.VMEM((OTHERS, 1, BLK), jnp.float32),
            pltpu.SMEM((8, PAIRS), jnp.int32),
            dma, dma, dma((CHUNKS,)), dma((PEERS,)), dma((PEERS,)), dma, dma, dma, dma, dma, dma((PEERS,)), dma,
            pltpu.SemaphoreType.REGULAR((2,)),
        ],
        compiler_params=pltpu.CompilerParams(
            collective_id=0, has_side_effects=True, vmem_limit_bytes=60 * 2**20),
        name="exchange",
    )(send_rows, pair_target, pair_slot, pair_target, src_area, tgt_area, src_field, weights)


HELD = 32


def finish_kernel(table, inb, weights, partial, ratio_ref, out, x, w, acc, scaled, xsem, wsem, asem, osem):
    load = pltpu.make_async_copy(partial, acc, asem)
    load.start()
    ranges = [(jnp.where(g == 0, 0, table[1, max(g * TB - 1, 0)]) + (ROOM[g] if g < GROUPS - 1 else 0),
               table[1, g * TB + TB - 1]) for g in range(GROUPS)]
    step = 8

    def copies(j, u):
        entry = table[0, j]
        slot = lax.shift_right_logical(entry, 6) & 255
        return (pltpu.make_async_copy(inb.at[slot], x.at[u], xsem),
                pltpu.make_async_copy(weights.at[lax.shift_right_logical(entry, 14)], w.at[u], wsem))

    def bring(lo, count):
        def one(u, _):
            for cp in copies(lo + u, u):
                cp.start()
            return 0

        lax.fori_loop(0, count, one, 0)

    def use(lo, count):
        def one(u, _):
            for cp in copies(lo + u, u):
                cp.wait()
            return 0

        lax.fori_loop(0, count, one, 0)

        def some(n, _):
            products = [jnp.dot(x[n * step + u], w[n * step + u], preferred_element_type=jnp.float32)
                        for u in range(step)]
            for u in range(step):
                i = n * step + u
                t = table[0, jnp.minimum(lo + i, PAIRS - 1)] & 63
                acc[t] = acc[t] + jnp.where(i < count, products[u], 0.0)
            return 0

        lax.fori_loop(0, lax.div(count + step - 1, step), some, 0)

    lo, hi = ranges[-1]
    count = jnp.minimum(hi - lo, HELD)
    bring(lo, count)
    ratio = jnp.broadcast_to(ratio_ref[...], (BLK, BLK)).T[:VREG]
    load.wait()
    use(lo, count)
    ranges[-1] = (lo + count, hi)
    for lo, hi in ranges:
        def more(n, _, lo=lo, hi=hi):
            first = lo + n * HELD
            count = jnp.minimum(hi - first, HELD)
            bring(first, count)
            use(first, count)
            return 0

        lax.fori_loop(0, lax.div(jnp.maximum(hi - lo, 0) + HELD - 1, HELD), more, 0)

    parts = 4
    per = TB // parts
    done = []
    for i in range(parts):
        for t in range(i * per, (i + 1) * per):
            scaled[:, t * BLK:(t + 1) * BLK] = acc[t] * ratio
        span = pl.ds(i * per * BLK, per * BLK)
        done.append(pltpu.make_async_copy(scaled.at[:, span], out.at[:, span], osem.at[i]))
        done[-1].start()
    for cp in done:
        cp.wait()


def finish(table, inb, weights, partial, ratio):
    smem = pl.BlockSpec(memory_space=pltpu.SMEM)
    vmem = pl.BlockSpec(memory_space=pltpu.VMEM)
    hbm = pl.BlockSpec(memory_space=pl.ANY)
    dma = pltpu.SemaphoreType.DMA
    return pl.pallas_call(
        finish_kernel,
        out_shape=jax.ShapeDtypeStruct((VREG, TB * BLK), jnp.float32),
        in_specs=[smem, hbm, hbm, hbm, vmem],
        out_specs=hbm,
        scratch_shapes=[
            pltpu.VMEM((HELD, VREG, BLK), jnp.bfloat16),
            pltpu.VMEM((HELD, BLK, BLK), jnp.bfloat16),
            pltpu.VMEM((TB, VREG, BLK), jnp.float32),
            pltpu.VMEM((VREG, TB * BLK), jnp.float32),
            dma, dma, dma, dma((4,)),
        ],
        compiler_params=pltpu.CompilerParams(vmem_limit_bytes=60 * 2**20),
        name="finish",
    )(table, inb, weights, partial, ratio)


def shards(src_field, src_area, tgt_area, weights, send_index, pair_slot, pair_target):
    inb, partial, table, ratio = exchange(
        send_index[0].T, pair_target, pair_slot, src_area.reshape(SB, BLK), tgt_area.reshape(TB, BLK), src_field, weights)
    return finish(table, inb.reshape(PEERS * CAP, VREG, BLK), weights, partial, ratio)


def solution(mesh):
    placed = (P(None, AXES), P(AXES), P(AXES), P(AXES, None, None), P(AXES, None, None), P(AXES), P(AXES))
    return jax.shard_map(shards, mesh=mesh, in_specs=placed, out_specs=P(None, AXES), check_vma=False)
```

time: 84.1 us -> 73.6 us (0.88)
  Pallas kernels: 82.7 us -> 72.8 us
  local copies, waits for them, and re-layouts: 1.24 us -> 0 us
    pallas_call x1, Pallas kernels: 17.8 us -> 5 us  [finish(): pl.pallas_call(finish_kernel, out_shape=jax.ShapeDtypeStruct((VREG, TB *...]
    pallas_call x1, Pallas kernels: 64.9 us -> 67.8 us  [exchange(): pl.pallas_call(exchange_kernel, out_shape=[jax.ShapeDtypeStruct((PEERS, C...]
    reshape x1 -> x0, local copies, waits for them, and re-layouts: 1.24 us -> none  [shards(): pair_slot.reshape(1, PAIRS)]
where the time goes in v3:
time: 73.6 us; the launch traced here: 72.8 us
  Pallas kernels  72.8 us (99%)
    pallas_call x1, Pallas kernels, exchange(): pl.pallas_call(exchange_kernel, out_shape=[jax.ShapeDtypeStruct((PEERS, C...  67.8 us
    pallas_call x1, Pallas kernels, finish(): pl.pallas_call(finish_kernel, out_shape=jax.ShapeDtypeStruct((VREG, TB *...  5 us

profile of v3, /device:TPU:1, one launch (start us, length us, event | category | flops | bytes accessed | tf_op | source)
XLA Modules:
  0.0 72.8 jit_solution(963393482359603756)
XLA Ops:
  0.0 67.8 %exchange.1 = (bf16[128,2,64,128]{3,2,1,0:T(8,128)(2,1)}, f32[64,64,128]{2,1,0:T(8,128)}, s32[8,384]{1,0:T(8,128)}, f32[1,128]{1,0:T(1,128)}) custom-call(s32[2,128]{1,0:T(2,128)} %bitcast.9, s32[384]{0:T(512)} %targets_ref.1, s32[384]{0:T(512)} %slots_ref.1, s32[384]{0:T(512)} %targets_ref.1, f32[256,128]{1,0:T(8,128)} %bitcast.7, f32[64,128]{1,0:T(8,128)} %bitcast.8, ...), custom_call_target="tpu_custom_call" | custom-call | tf_op jit(solution)/shard_map/exchange/pallas_call | solution.py:322
  67.8 5.0 %finish.1 = f32[64,8192]{1,0:T(8,128)} custom-call(s32[8,384]{1,0:T(8,128)} %get-tuple-element.9.table, bf16[256,64,128]{2,1,0:T(8,128)(2,1)} %bitcast.6, bf16[384,128,128]{2,1,0:T(8,128)(2,1)} %weights.3, f32[64,64,128]{2,1,0:T(8,128)} %get-tuple-element.11.partial, f32[1,128]{1,0:T(1,128)} %get-tuple-element.12.ratio_ref), custom_call_target="tpu_custom_call" | custom-call | tf_op jit(solution)/shard_map/finish/pallas_call | solution.py:432

commit v4 on v3

--- a/solution.py
+++ b/solution.py
@@ -51,7 +51,7 @@
 ORDER = offsets_in_order()
 GROUPS = 5
 ENDS = [sum(group_of(o) <= g for o in ORDER) for g in range(GROUPS)]
-FIRST = 90
+FIRST = 86
 ROOM = (160, 96, 96, 80)
 NEAR = [o for o in ORDER if sum(v != 0 for v in o) == 1]
 PLANE = [o for o in ORDER if o[2] == 0 and o[3] == 0]

time: 73.6 us -> 74.8 us (1.016)
  the two profiles are of different devices: /device:TPU:1 before, /device:TPU:22 now
where the time goes in v4:
time: 74.8 us; the launch traced here: 73.5 us
  Pallas kernels  73.5 us (98%)
    pallas_call x1, Pallas kernels, exchange(): pl.pallas_call(exchange_kernel, out_shape=[jax.ShapeDtypeStruct((PEERS, C...  68.5 us
    pallas_call x1, Pallas kernels, finish(): pl.pallas_call(finish_kernel, out_shape=jax.ShapeDtypeStruct((VREG, TB *...  4.99 us

profile of v4, /device:TPU:22, one launch (start us, length us, event | category | flops | bytes accessed | tf_op | source)
XLA Modules:
  0.0 73.5 jit_solution(5865721005457450358)
XLA Ops:
  0.0 68.5 %exchange.1 = (bf16[128,2,64,128]{3,2,1,0:T(8,128)(2,1)}, f32[64,64,128]{2,1,0:T(8,128)}, s32[8,384]{1,0:T(8,128)}, f32[1,128]{1,0:T(1,128)}) custom-call(s32[2,128]{1,0:T(2,128)} %bitcast.9, s32[384]{0:T(512)} %targets_ref.1, s32[384]{0:T(512)} %slots_ref.1, s32[384]{0:T(512)} %targets_ref.1, f32[256,128]{1,0:T(8,128)} %bitcast.7, f32[64,128]{1,0:T(8,128)} %bitcast.8, ...), custom_call_target="tpu_custom_call" | custom-call | tf_op jit(solution)/shard_map/exchange/pallas_call | solution.py:322
  68.5 5.0 %finish.1 = f32[64,8192]{1,0:T(8,128)} custom-call(s32[8,384]{1,0:T(8,128)} %get-tuple-element.9.table, bf16[256,64,128]{2,1,0:T(8,128)(2,1)} %bitcast.6, bf16[384,128,128]{2,1,0:T(8,128)(2,1)} %weights.3, f32[64,64,128]{2,1,0:T(8,128)} %get-tuple-element.11.partial, f32[1,128]{1,0:T(1,128)} %get-tuple-element.12.ratio_ref), custom_call_target="tpu_custom_call" | custom-call | tf_op jit(solution)/shard_map/finish/pallas_call | solution.py:432
